TPU v7x, 32 devices: a whole 2x2x4 slice. The times are simulated.
32 devices in a mesh: dp: 8 (over z, x), mp: 4 (over y, core).
Axes of the slice: x: 2, y: 2, z: 4, core: 2. Of those that a mesh axis runs over, the one named last changes fastest.
Arguments:
- grad_tiles: bfloat16 [16, 512, 512], P(None, 'dp', 'mp'), may hold values from -8 to 8
- factor_stats: float32 [16, 2, 512, 512], P('dp', None, 'mp'), may hold values from -80 to 500, as said below
- owner_blocks: int32 [8, 2], replicated, may hold values from 0 to 15, as said below
- rotation: int32 [1], replicated, may hold values from 0 to 7
Outputs:
- preconditioned: bfloat16 [16, 512, 512], P(None, 'dp', 'mp')
- new_stats: float32 [16, 2, 512, 512], P('dp', None, 'mp')
Inputs may be any that keep to these rules, and one draw needn't show every extreme that they name: Each matrix factor_stats[slot, side] is symmetric and positive definite. `owner_blocks`: every block number 0 to 15 stands exactly once.
All inputs are finite; a program needn't handle non-finite values.
Results may differ from a plain program's by a relative error of at most 0.0092.
Values may be sent and summed in bfloat16 or wider, within the bound.
No kernel may reach another device: no remote copies, remote signals or barrier semaphores. Data moves between devices by JAX's collectives and lax.ppermute only.
A program may use at most 64 MiB of HBM per device.

v0:
```python
import jax
import jax.numpy as jnp
from jax import lax
from jax.sharding import PartitionSpec as P

ITERS = 2
decay_rate = 0.9
damping = 1.0


def newton_root(factor):
    order = factor.shape[-1]
    identity = jnp.eye(order, dtype=jnp.float32)
    squares = jnp.sum(jnp.square(factor.astype(jnp.float32)), axis=(1, 2), keepdims=True)
    norm_scale = 2.5 / jnp.sqrt(squares)
    moment = (norm_scale * factor.astype(jnp.float32)).astype(jnp.bfloat16)
    current = None
    for newton_step in range(ITERS):
        step_t = ((5.0 * identity - moment.astype(jnp.float32)) * 0.25).astype(jnp.bfloat16)
        if newton_step == 0:
            current = step_t
        else:
            current = jnp.einsum(
                "sij,sjk->sik", current, step_t, preferred_element_type=jnp.float32
            ).astype(jnp.bfloat16)
        if newton_step + 1 < ITERS:
            square = jnp.einsum(
                "sij,sjk->sik", step_t, step_t, preferred_element_type=jnp.float32
            ).astype(jnp.bfloat16)
            partial_m = jnp.einsum(
                "sij,sjk->sik", square, moment, preferred_element_type=jnp.float32
            ).astype(jnp.bfloat16)
            moment = jnp.einsum(
                "sij,sjk->sik", square, partial_m, preferred_element_type=jnp.float32
            ).astype(jnp.bfloat16)
    return current


def body(grad_tiles, factor_stats, owner_blocks, rotation):
    dp_count = lax.axis_size("dp")
    mp_count = lax.axis_size("mp")
    block_count = grad_tiles.shape[0]
    tile_rows = grad_tiles.shape[1]
    tile_cols = grad_tiles.shape[2]
    slots = owner_blocks.shape[1]
    rows_each = factor_stats.shape[2]
    order = factor_stats.shape[3]
    per_slot = mp_count // slots
    part_width = order // per_slot
    my_index = lax.axis_index("mp")
    my_slot = my_index // per_slot
    my_part = my_index % per_slot
    owners = jnp.roll(owner_blocks, rotation[0], axis=0)
    outgoing = jnp.take(grad_tiles, owners.T, axis=0)
    arrived = lax.all_to_all(outgoing, "dp", split_axis=1, concat_axis=1, tiled=True)
    col_part = arrived.reshape(slots, order, tile_cols)
    blocks = lax.all_gather(col_part, "mp", axis=2, tiled=True)
    row_part = lax.dynamic_slice_in_dim(blocks, my_index * rows_each, rows_each, 1)
    left_rows = jnp.einsum("kij,klj->kil", row_part, blocks, preferred_element_type=jnp.float32)
    right_rows = jnp.einsum("kji,kjl->kil", col_part, blocks, preferred_element_type=jnp.float32)
    fresh_rows = jnp.stack([left_rows, right_rows], axis=1)
    new_stats = decay_rate * factor_stats + (1.0 - decay_rate) * fresh_rows
    row_ids = my_index * rows_each + jnp.arange(rows_each)
    identity_rows = (row_ids[:, None] == jnp.arange(order)[None, :]).astype(jnp.float32)
    factor_rows = (new_stats + damping * identity_rows).astype(jnp.bfloat16)
    spread_rows = jnp.repeat(factor_rows, per_slot, axis=0)
    factor = lax.all_to_all(spread_rows, "mp", split_axis=0, concat_axis=2, tiled=True)[0]
    inverse_roots = newton_root(factor)
    grad_block = lax.dynamic_index_in_dim(blocks, my_slot, 0, keepdims=False)
    right_part = lax.dynamic_slice_in_dim(inverse_roots[1], my_part * part_width, part_width, 1)
    right_applied = jnp.dot(grad_block, right_part, preferred_element_type=jnp.float32).astype(
        jnp.bfloat16
    )
    result = jnp.dot(inverse_roots[0], right_applied, preferred_element_type=jnp.float32).astype(
        jnp.bfloat16
    )
    all_parts = lax.all_gather(result, "mp", axis=1, tiled=True)
    slot_parts = all_parts.reshape(order, slots, order)
    grad_squares = jnp.sum(jnp.square(blocks.astype(jnp.float32)), axis=(1, 2))
    result_squares = jnp.sum(jnp.square(slot_parts.astype(jnp.float32)), axis=(0, 2))
    graft_scale = jnp.sqrt(grad_squares) / (jnp.sqrt(result_squares) + 1e-06)
    my_cols = lax.dynamic_slice_in_dim(slot_parts, my_index * tile_cols, tile_cols, 2)
    scaled = (my_cols.astype(jnp.float32) * graft_scale[None, :, None]).astype(jnp.bfloat16)
    outgoing_back = scaled.reshape(dp_count, tile_rows, slots, tile_cols)
    returned = lax.all_to_all(outgoing_back, "dp", split_axis=0, concat_axis=0, tiled=True)
    owner_flat = owners.reshape(-1)
    position = (
        jnp.zeros((block_count,), jnp.int32)
        .at[owner_flat]
        .set(jnp.arange(owner_flat.shape[0], dtype=jnp.int32))
    )
    holder_row = position // slots
    holder_slot = position % slots
    preconditioned = returned[holder_row, :, holder_slot, :]
    return (preconditioned, new_stats)


def solution(mesh):
    return jax.shard_map(
        body,
        mesh=mesh,
        in_specs=(P(None, "dp", "mp"), P("dp", None, "mp", None), P(), P()),
        out_specs=(P(None, "dp", "mp"), P("dp", None, "mp", None)),
        check_vma=False,
    )
```

profile of v0, /device:TPU:0, one launch (start us, length us, event | category | flops | bytes accessed | tf_op | source)
XLA Modules:
  0.0 122.4 jit_solution(869235592168875510)
XLA Ops:
  7.2 0.0 copy-start
  7.2 0.0 all-gather.3.cloned.1.call-start
  7.9 0.8 pad_add_fusion
  8.8 0.1 compare_and_fusion
  8.8 0.1 reshape.116
  8.9 0.6 gather_fusion
  9.5 0.1 broadcast_select_fusion
  9.7 16.0 %all_to_all.19 = bf16[2,8,64,128]{3,2,0,1:T(8,128)(2,1)S(1)} all-to-all(bf16[2,8,64,128]{3,2,0,1:T(8,128)(2,1)S(1)} %copy.41), channel_id=1, replica_groups=mesh['dp'=8,'mp'=4] {'dp'}, dimensions={1} | all-to-all | bytes 524288 | tf_op jit(solution)/shard_map/all_to_all | solution.py:55
  25.7 0.7 copy.42
  26.4 0.0 all-gather.3.cloned.1.call-update
  26.4 0.8 fusion.12
  27.2 15.2 %all-gather.3.cloned.1.call-done = bf16[2,512,512]{2,1,0:T(8,128)(2,1)} async-done(((bf16[2,512,128]{2,1,0:T(8,128)(2,1)}), bf16[2,512,512]{2,1,0:T(8,128)(2,1)}) %all-gather.3.cloned.1.call-update) | async-done | bytes 1048592 | tf_op jit(solution)/shard_map/all_gather | solution.py:57
  42.4 1.7 %convolution_bitcast_fusion = f32[2,1,128,512]{3,2,0,1:T(8,128)S(1)} fusion(bf16[2,512,128]{2,1,0:T(8,128)(2,1)} %bitcast.43, bf16[2,512,512]{2,1,0:T(8,128)(2,1)} %all-gather.3.cloned.1.call-done), kind=kOutput, calls=%fused_computation.15 | convolution fusion | flops 134217728 | bytes 1835008 | tf_op jit(solution)/shard_map/kji,kjl->kil/dot_general | solution.py:60
  44.2 0.5 convolution_bitcast_fusion.1
  44.7 0.3 add_convert_fusion
  45.0 1.1 broadcast_in_dim.32
  46.1 3.5 %all-to-all-start.1 = ((bf16[4,2,128,512]{3,2,1,0:T(8,128)(2,1)}), bf16[4,2,128,512]{3,2,1,0:T(8,128)(2,1)S(1)}, u32[]{:S(2)}, u32[]{:S(2)}) async-start(bf16[4,2,128,512]{3,2,1,0:T(8,128)(2,1)} %bitcast.6), calls=%async_computation.1 | async-start | bytes 2097152 | tf_op jit(solution)/shard_map/all_to_all | solution.py:67
  49.6 0.0 all-gather.5.cloned.1.call-start
  49.7 1.2 fusion.2
  50.9 13.2 %all-to-all-done.1 = bf16[4,2,128,512]{3,2,1,0:T(8,128)(2,1)S(1)} async-done(((bf16[4,2,128,512]{3,2,1,0:T(8,128)(2,1)}), bf16[4,2,128,512]{3,2,1,0:T(8,128)(2,1)S(1)}, u32[]{:S(2)}, u32[]{:S(2)}) %all-to-all-start.1) | async-done | bytes 1048608 | tf_op jit(solution)/shard_map/all_to_all | solution.py:67
  64.0 0.3 convert_bitcast_fusion
  64.3 0.2 copy.45
  64.5 0.4 fusion
  64.9 0.3 multiply_convert_fusion.2
  65.3 1.0 copy-done.4
  66.2 0.0 copy-done.2
  66.2 1.7 %convolution_convert_fusion.3 = bf16[2,512,512]{2,1,0:T(8,128)(2,1)} fusion(bf16[2,512,512]{2,1,0:T(8,128)(2,1)S(1)} %multiply_convert_fusion.2, f32[512,512]{1,0:T(8,128)S(1)} %copy-done.2), kind=kOutput, calls=%fused_computation.14 | convolution fusion | flops 539492352 | bytes 3145728 | tf_op jit(solution)/shard_map/sij,sjk->sik/dot_general | solution.py:27
  67.9 4.2 %multiply_convert_fusion = bf16[2,512,512]{2,1,0:T(8,128)(2,1)} fusion(bf16[2,512,512]{2,1,0:T(8,128)(2,1)} %convolution_convert_fusion.3, bf16[2,512,512]{2,1,0:T(8,128)(2,1)} %copy-done.4, f32[512,512]{1,0:T(8,128)S(1)} %copy-done.3), kind=kOutput, calls=%fused_computation.8 | convolution fusion | flops 1076887552 | bytes 4194304 | tf_op jit(solution)/shard_map/sij,sjk->sik/dot_general | solution.py:33
  72.2 2.3 %convolution_convert_fusion = bf16[2,512,512]{2,1,0:T(8,128)(2,1)S(1)} fusion(bf16[2,512,512]{2,1,0:T(8,128)(2,1)} %multiply_convert_fusion, bf16[2,512,512]{2,1,0:T(8,128)(2,1)} %copy-done.4, f32[512,512]{1,0:T(8,128)S(1)} %copy-done.3), kind=kOutput, calls=%fused_computation.11 | convolution fusion | flops 539492352 | bytes 4194304 | tf_op jit(solution)/shard_map/sij,sjk->sik/dot_general | solution.py:23
  74.4 0.0 copy-start.7
  74.4 1.0 copy-done.7
  75.4 2.5 %convolution_convert_fusion.4 = bf16[512,256]{1,0:T(8,128)(2,1)} fusion(bf16[2,512,512]{2,1,0:T(8,128)(2,1)} %copy-done.7, bf16[2,512,512]{2,1,0:T(8,128)(2,1)S(1)} %copy-done.1, s32[]{:T(128)S(6)} %select_n.76, bf16[1,512,512]{2,1,0:T(8,128)(2,1)S(1)} %slice.13, s32[]{:T(128)S(6)} %select_n.78), kind=kOutput, calls=%fused_computation.17 | convolution fusion | flops 268697600 | bytes 1572872 | tf_op jit(solution)/shard_map/dot_general | solution.py:74
  77.9 0.0 all-gather.5.cloned.1.call-update
  78.0 0.4 multiply_reduce_fusion.1
  78.3 16.6 %all-gather.5.cloned.1.call-done = bf16[512,1024]{1,0:T(8,128)(2,1)} async-done(((bf16[512,256]{1,0:T(8,128)(2,1)}), bf16[512,1024]{1,0:T(8,128)(2,1)}) %all-gather.5.cloned.1.call-update) | async-done | bytes 1048592 | tf_op jit(solution)/shard_map/all_gather | solution.py:77
  94.9 1.5 %multiply_reduce_fusion = f32[1024]{0:T(1024)S(1)} fusion(bf16[512,1024]{1,0:T(8,128)(2,1)} %all-gather.5.cloned.1.call-done), kind=kLoop, calls=%fused_computation.6 | loop fusion | flops 1571840 | bytes 1052672 | tf_op jit(solution)/shard_map/reduce_sum | solution.py:80
  96.4 1.8 %reshape.109 = bf16[512,2,512]{2,1,0:T(2,128)(2,1)S(1)} reshape(bf16[512,1024]{1,0:T(8,128)(2,1)} %all-gather.5.cloned.1.call-done) | data formatting | bytes 2097152 | tf_op jit(solution)/shard_map/reshape | solution.py:78
  98.3 0.2 constant_dynamic-slice_fusion
  98.5 0.1 reduce_sum.38
  98.6 0.1 multiply_convert_fusion.3
  98.7 0.7 copy.47
  99.4 5.5 %all-to-all-start.2 = ((bf16[8,64,2,128]{3,1,2,0:T(8,128)(2,1)}), bf16[8,64,2,128]{3,1,2,0:T(8,128)(2,1)S(1)}, u32[]{:S(2)}, u32[]{:S(2)}) async-start(bf16[8,64,2,128]{3,1,2,0:T(8,128)(2,1)} %copy.47), calls=%async_computation.2 | async-start | bytes 524288 | tf_op jit(solution)/shard_map/all_to_all | solution.py:85
  105.0 0.1 copy.48
  105.0 0.1 reshape.111
  105.1 0.6 scatter_custom_fusion
  105.8 1.0 copy.49
  106.8 7.5 %all-to-all-done.2 = bf16[8,64,2,128]{3,1,2,0:T(8,128)(2,1)S(1)} async-done(((bf16[8,64,2,128]{3,1,2,0:T(8,128)(2,1)}), bf16[8,64,2,128]{3,1,2,0:T(8,128)(2,1)S(1)}, u32[]{:S(2)}, u32[]{:S(2)}) %all-to-all-start.2) | async-done | bytes 262176 | tf_op jit(solution)/shard_map/all_to_all | solution.py:85
  114.3 1.3 %gather_fusion.1 = bf16[16,64,128]{2,1,0:T(8,128)(2,1)} fusion(bf16[8,64,2,128]{3,1,2,0:T(8,128)(2,1)S(1)} %all-to-all-done.2, s32[16]{0:T(128)S(1)} %fusion.19), kind=kCustom, calls=%fused_computation.1 | custom fusion | bytes 524416 | tf_op jit(solution)/shard_map/gather | solution.py:94
  (23 shorter events, 0.2 us)
Async XLA Ops:
  7.2 1.8 %copy-start = (bf16[16,64,128]{2,1,0:T(8,128)(2,1)S(1)}, bf16[16,64,128]{2,1,0:T(8,128)(2,1)}, u32[]{:S(2)}) copy-start(bf16[16,64,128]{2,1,0:T(8,128)(2,1)} %param.4) | copy-start | bytes 786436
  7.2 35.2 %all-gather.3.cloned.1.call-start = ((), (), s32[]{:S(2)}) async-start(), calls=%async_computation.3 | async-start | bytes 1310720 | tf_op jit(solution)/shard_map/all_gather | solution.py:57
  26.4 18.3 %copy-start.5 = (f32[2,2,128,512]{3,2,1,0:T(8,128)S(1)}, f32[2,2,128,512]{3,2,1,0:T(8,128)}, u32[]{:S(2)}) copy-start(f32[2,2,128,512]{3,2,1,0:T(8,128)} %param.5) | copy-start | bytes 3145732
  42.4 1.8 %copy-start.1 = (bf16[2,512,512]{2,1,0:T(8,128)(2,1)S(1)}, bf16[2,512,512]{2,1,0:T(8,128)(2,1)}, u32[]{:S(2)}) copy-start(bf16[2,512,512]{2,1,0:T(8,128)(2,1)} %all-gather.3.cloned.1.call-done) | copy-start | bytes 3145732
  42.4 2.3 %copy-start.6 = (f32[128,512]{1,0:T(8,128)S(1)}, f32[128,512]{1,0:T(8,128)}, u32[]{:S(2)}) copy-start(f32[128,512]{1,0:T(8,128)} %fusion.12) | copy-start | bytes 786436
  46.1 17.9 %all-to-all-start.1 = ((bf16[4,2,128,512]{3,2,1,0:T(8,128)(2,1)}), bf16[4,2,128,512]{3,2,1,0:T(8,128)(2,1)S(1)}, u32[]{:S(2)}, u32[]{:S(2)}) async-start(bf16[4,2,128,512]{3,2,1,0:T(8,128)(2,1)} %bitcast.6), calls=%async_computation.1 | async-start | bytes 2097152 | tf_op jit(solution)/shard_map/all_to_all | solution.py:67
  49.6 45.3 %all-gather.5.cloned.1.call-start = ((), (), s32[]{:S(2)}) async-start(), calls=%async_computation.4 | async-start | bytes 1310720 | tf_op jit(solution)/shard_map/all_gather | solution.py:77
  64.5 1.7 %copy-start.2 = (f32[512,512]{1,0:T(8,128)S(1)}, f32[512,512]{1,0:T(8,128)}, u32[]{:S(2)}) copy-start(f32[512,512]{1,0:T(8,128)} %fusion.2) | copy-start | bytes 3145732
  65.2 1.0 copy-start.4
  66.2 1.7 %copy-start.3 = (f32[512,512]{1,0:T(8,128)S(1)}, f32[512,512]{1,0:T(8,128)}, u32[]{:S(2)}) copy-start(f32[512,512]{1,0:T(8,128)} %fusion.2) | copy-start | bytes 3145732
  74.4 1.0 copy-start.7
  99.4 14.8 %all-to-all-start.2 = ((bf16[8,64,2,128]{3,1,2,0:T(8,128)(2,1)}), bf16[8,64,2,128]{3,1,2,0:T(8,128)(2,1)S(1)}, u32[]{:S(2)}, u32[]{:S(2)}) async-start(bf16[8,64,2,128]{3,1,2,0:T(8,128)(2,1)} %copy.47), calls=%async_computation.2 | async-start | bytes 524288 | tf_op jit(solution)/shard_map/all_to_all | solution.py:85
Sparse Core Ops, SparseCore 0:
  26.5 15.8 all-gather.2
  78.1 16.8 all-gather.4
where the time goes:
time: 123 us; the launch traced here: 122 us
  waiting for transfers between devices  52.4 us (43%)
  blocking collectives  16 us (13%)
  between operations  15 us (12%)
  matrix products  12.9 us (10%)
  local copies, waits for them, and re-layouts  10.6 us (9%)
  starting transfers between devices  9.11 us (7%)
  other arithmetic  6.43 us (5%)
    all_gather x1, waiting for transfers between devices, body(): all_parts = lax.all_gather(result, 'mp', axis=1, tiled=True)  16.6 us
    all_to_all x1, blocking collectives, body(): lax.all_to_all(outgoing, 'dp', split_axis=1, concat_axis=1, tiled=True)  16 us
    all_gather x1, waiting for transfers between devices, body(): blocks = lax.all_gather(col_part, 'mp', axis=2, tiled=True)  15.2 us
    all_to_all x1, waiting for transfers between devices, body(): lax.all_to_all(spread_rows, 'mp', split_axis=0, concat_axis=2, tiled=True)  13.2 us
    all_to_all x1, waiting for transfers between devices, body(): lax.all_to_all(outgoing_back, 'dp', split_axis=0, concat_axis=0, tiled=True)  7.46 us
    all_to_all x1, starting transfers between devices, body(): lax.all_to_all(outgoing_back, 'dp', split_axis=0, concat_axis=0, tiled=True)  5.51 us
    dot_general x1, matrix products, newton_root(): jnp.einsum('sij,sjk->sik', square, partial_m, preferred_element_type=jnp....  4.21 us
    all_to_all x1, starting transfers between devices, body(): lax.all_to_all(spread_rows, 'mp', split_axis=0, concat_axis=2, tiled=True)  3.52 us
  transfers between devices with their start and end apart: 4, of which 4 were waited for; matrix products, arithmetic and copies ran while one was open for 3% of the time, Pallas kernels for 0%

commit v1 on v0

--- a/solution.py
+++ b/solution.py
@@ -6,6 +6,22 @@
 ITERS = 2
 decay_rate = 0.9
 damping = 1.0
+
+
+def swapped_with_each(x, axis, split, join):
+    ways, here = (lax.axis_size(axis), lax.axis_index(axis))
+    width = x.shape[split] // ways
+    dims = list(x.shape)
+    dims[split] = width
+    height = dims[join]
+    dims[join] = height * ways
+    full = jnp.zeros(dims, x.dtype)
+    for mask in range(ways):
+        part = lax.dynamic_slice_in_dim(x, (here ^ mask) * width, width, axis=split)
+        if mask:
+            part = lax.ppermute(part, axis, [(d, d ^ mask) for d in range(ways)])
+        full = lax.dynamic_update_slice_in_dim(full, part, (here ^ mask) * height, axis=join)
+    return full
 
 
 def newton_root(factor):
@@ -52,7 +68,7 @@
     my_part = my_index % per_slot
     owners = jnp.roll(owner_blocks, rotation[0], axis=0)
     outgoing = jnp.take(grad_tiles, owners.T, axis=0)
-    arrived = lax.all_to_all(outgoing, "dp", split_axis=1, concat_axis=1, tiled=True)
+    arrived = swapped_with_each(outgoing, "dp", 1, 1)
     col_part = arrived.reshape(slots, order, tile_cols)
     blocks = lax.all_gather(col_part, "mp", axis=2, tiled=True)
     row_part = lax.dynamic_slice_in_dim(blocks, my_index * rows_each, rows_each, 1)

time: 123 us -> 124 us (level)
  blocking collectives: 16 us -> 0 us
  starting transfers between devices: 9.11 us -> 21.7 us
  waiting for transfers between devices: 52.4 us -> 57.2 us
    all_to_all x1 -> x0, blocking collectives: 16 us -> none  [body(): lax.all_to_all(outgoing, 'dp', split_axis=1, concat_axis=1, tiled=True)]
    ppermute x0 -> x7, starting transfers between devices: none -> 12.6 us  [swapped_with_each(): part = lax.ppermute(part, axis, [(d, d ^ mask) for d in range(ways)])]
    ppermute x0 -> x7, waiting for transfers between devices: none -> 6.49 us  [swapped_with_each(): part = lax.ppermute(part, axis, [(d, d ^ mask) for d in range(ways)])]
    all_gather x1, waiting for transfers between devices: 15.2 us -> 13.5 us  [body(): blocks = lax.all_gather(col_part, 'mp', axis=2, tiled=True)]
    unnamed x17 -> x19, local copies, waits for them, and re-layouts: 3 us -> 3.71 us
  transfers between devices with their start and end apart: 4 -> 11, of which waited for: 4 -> 7; matrix products, arithmetic and copies ran while one was open for 3% -> 3% of each run, Pallas kernels for 0% -> 0%
where the time goes in v1:
time: 124 us
  waiting for transfers between devices  57.2 us (46%)
  starting transfers between devices  21.7 us (18%)
  between operations  15.1 us (12%)
  matrix products  12.8 us (10%)
  local copies, waits for them, and re-layouts  10.7 us (9%)
  other arithmetic  6.38 us (5%)
    all_gather x1, waiting for transfers between devices, body(): all_parts = lax.all_gather(result, 'mp', axis=1, tiled=True)  16.6 us
    all_gather x1, waiting for transfers between devices, body(): blocks = lax.all_gather(col_part, 'mp', axis=2, tiled=True)  13.5 us
    all_to_all x1, waiting for transfers between devices, body(): lax.all_to_all(spread_rows, 'mp', split_axis=0, concat_axis=2, tiled=True)  13.2 us
    ppermute x7, starting transfers between devices, swapped_with_each(): part = lax.ppermute(part, axis, [(d, d ^ mask) for d in range(ways)])  12.6 us
    all_to_all x1, waiting for transfers between devices, body(): lax.all_to_all(outgoing_back, 'dp', split_axis=0, concat_axis=0, tiled=True)  7.46 us
    ppermute x7, waiting for transfers between devices, swapped_with_each(): part = lax.ppermute(part, axis, [(d, d ^ mask) for d in range(ways)])  6.49 us
    all_to_all x1, starting transfers between devices, body(): lax.all_to_all(outgoing_back, 'dp', split_axis=0, concat_axis=0, tiled=True)  5.51 us
    dot_general x1, matrix products, newton_root(): jnp.einsum('sij,sjk->sik', square, partial_m, preferred_element_type=jnp....  4.15 us
  transfers between devices with their start and end apart: 11, of which 7 were waited for; matrix products, arithmetic and copies ran while one was open for 3% of the time, Pallas kernels for 0%

profile of v1, /device:TPU:0, one launch (start us, length us, event | category | flops | bytes accessed | tf_op | source)
XLA Modules:
  0.0 123.9 jit_solution(9680982481323596238)
XLA Ops:
  8.0 0.8 pad_add_fusion
  8.8 0.1 compare_and_fusion
  8.9 0.1 reshape.116
  9.0 0.6 gather_fusion
  9.6 0.1 broadcast_select_fusion
  9.8 3.0 %collective-permute-start = (bf16[2,1,64,128]{3,2,1,0:T(8,128)(2,1)S(1)}, bf16[2,1,64,128]{3,2,1,0:T(8,128)(2,1)S(1)}, u32[]{:S(2)}, u32[]{:S(2)}) collective-permute-start(bf16[2,1,64,128]{3,2,1,0:T(8,128)(2,1)S(1)} %get-tuple-element.22), channel_id=1, source_target_pairs={{0,4},{4,0},{8,12},{12,8},{16,20},{20,16},{24,28},{28,24},{1,5},{5... | collective-permute-start | bytes 98312 | tf_op jit(solution)/shard_map/ppermute | solution.py:22
  12.8 1.6 %collective-permute-start.1 = (bf16[2,1,64,128]{3,2,1,0:T(8,128)(2,1)S(1)}, bf16[2,1,64,128]{3,2,1,0:T(8,128)(2,1)S(1)}, u32[]{:S(2)}, u32[]{:S(2)}) collective-permute-start(bf16[2,1,64,128]{3,2,1,0:T(8,128)(2,1)S(1)} %get-tuple-element.21), channel_id=1, source_target_pairs={{0,8},{4,12},{8,0},{12,4},{16,24},{20,28},{24,16},{28,20},{1,9},{5... | collective-permute-start | bytes 98312 | tf_op jit(solution)/shard_map/ppermute | solution.py:22
  14.4 3.0 %collective-permute-start.3 = (bf16[2,1,64,128]{3,2,1,0:T(8,128)(2,1)S(1)}, bf16[2,1,64,128]{3,2,1,0:T(8,128)(2,1)S(1)}, u32[]{:S(2)}, u32[]{:S(2)}) collective-permute-start(bf16[2,1,64,128]{3,2,1,0:T(8,128)(2,1)S(1)} %get-tuple-element.19), channel_id=1, source_target_pairs={{0,16},{4,20},{8,24},{12,28},{16,0},{20,4},{24,8},{28,12},{1,17},{... | collective-permute-start | bytes 98312 | tf_op jit(solution)/shard_map/ppermute | solution.py:22
  17.4 1.3 %collective-permute-start.4 = (bf16[2,1,64,128]{3,2,1,0:T(8,128)(2,1)S(1)}, bf16[2,1,64,128]{3,2,1,0:T(8,128)(2,1)S(1)}, u32[]{:S(2)}, u32[]{:S(2)}) collective-permute-start(bf16[2,1,64,128]{3,2,1,0:T(8,128)(2,1)S(1)} %get-tuple-element.18), channel_id=1, source_target_pairs={{0,20},{4,16},{8,28},{12,24},{16,4},{20,0},{24,12},{28,8},{1,21},{... | collective-permute-start | bytes 98312 | tf_op jit(solution)/shard_map/ppermute | solution.py:22
  18.7 3.6 %collective-permute-start.5 = (bf16[2,1,64,128]{3,2,1,0:T(8,128)(2,1)S(1)}, bf16[2,1,64,128]{3,2,1,0:T(8,128)(2,1)S(1)}, u32[]{:S(2)}, u32[]{:S(2)}) collective-permute-start(bf16[2,1,64,128]{3,2,1,0:T(8,128)(2,1)S(1)} %get-tuple-element.17), channel_id=1, source_target_pairs={{0,24},{4,28},{8,16},{12,20},{16,8},{20,12},{24,0},{28,4},{1,25},{... | collective-permute-start | bytes 98312 | tf_op jit(solution)/shard_map/ppermute | solution.py:22
  22.5 0.8 collective-permute-done.4
  23.3 1.3 %collective-permute-done.5 = bf16[2,1,64,128]{3,2,1,0:T(8,128)(2,1)S(1)} collective-permute-done((bf16[2,1,64,128]{3,2,1,0:T(8,128)(2,1)S(1)}, bf16[2,1,64,128]{3,2,1,0:T(8,128)(2,1)S(1)}, u32[]{:S(2)}, u32[]{:S(2)}) %collective-permute-start.5) | collective-permute-done | bytes 32800 | tf_op jit(solution)/shard_map/ppermute | solution.py:22
  24.5 4.4 %collective-permute-done.6 = bf16[2,1,64,128]{3,2,1,0:T(8,128)(2,1)S(1)} collective-permute-done((bf16[2,1,64,128]{3,2,1,0:T(8,128)(2,1)S(1)}, bf16[2,1,64,128]{3,2,1,0:T(8,128)(2,1)S(1)}, u32[]{:S(2)}, u32[]{:S(2)}) %collective-permute-start.6) | collective-permute-done | bytes 32800 | tf_op jit(solution)/shard_map/ppermute | solution.py:22
  29.0 0.7 copy-done.2
  29.7 0.8 fusion.12
  30.5 13.5 %all-gather.3.cloned.1.call-done = bf16[2,512,512]{2,1,0:T(8,128)(2,1)} async-done(((bf16[2,512,128]{2,1,0:T(8,128)(2,1)}), bf16[2,512,512]{2,1,0:T(8,128)(2,1)}) %all-gather.3.cloned.1.call-update) | async-done | bytes 1048592 | tf_op jit(solution)/shard_map/all_gather | solution.py:73
  44.0 1.7 %convolution_bitcast_fusion = f32[2,1,128,512]{3,2,0,1:T(8,128)S(1)} fusion(bf16[2,512,128]{2,1,0:T(8,128)(2,1)} %bitcast.43, bf16[2,512,512]{2,1,0:T(8,128)(2,1)} %all-gather.3.cloned.1.call-done), kind=kOutput, calls=%fused_computation.15 | convolution fusion | flops 134217728 | bytes 1835008 | tf_op jit(solution)/shard_map/kji,kjl->kil/dot_general | solution.py:76
  45.8 0.5 convolution_bitcast_fusion.1
  46.3 0.3 add_convert_fusion
  46.6 1.1 broadcast_in_dim.36
  47.7 3.5 %all-to-all-start = ((bf16[4,2,128,512]{3,2,1,0:T(8,128)(2,1)}), bf16[4,2,128,512]{3,2,1,0:T(8,128)(2,1)S(1)}, u32[]{:S(2)}, u32[]{:S(2)}) async-start(bf16[4,2,128,512]{3,2,1,0:T(8,128)(2,1)} %bitcast.6), calls=%async_computation | async-start | bytes 2097152 | tf_op jit(solution)/shard_map/all_to_all | solution.py:83
  51.3 1.1 fusion.2
  52.4 13.2 %all-to-all-done = bf16[4,2,128,512]{3,2,1,0:T(8,128)(2,1)S(1)} async-done(((bf16[4,2,128,512]{3,2,1,0:T(8,128)(2,1)}), bf16[4,2,128,512]{3,2,1,0:T(8,128)(2,1)S(1)}, u32[]{:S(2)}, u32[]{:S(2)}) %all-to-all-start) | async-done | bytes 1048608 | tf_op jit(solution)/shard_map/all_to_all | solution.py:83
  65.6 0.3 convert_bitcast_fusion
  65.9 0.2 copy.31
  66.1 0.4 fusion
  66.5 0.3 multiply_convert_fusion.2
  66.8 1.0 copy-done.5
  67.8 1.7 %convolution_convert_fusion.3 = bf16[2,512,512]{2,1,0:T(8,128)(2,1)} fusion(bf16[2,512,512]{2,1,0:T(8,128)(2,1)S(1)} %multiply_convert_fusion.2, f32[512,512]{1,0:T(8,128)S(1)} %copy-done.3), kind=kOutput, calls=%fused_computation.14 | convolution fusion | flops 539492352 | bytes 3145728 | tf_op jit(solution)/shard_map/sij,sjk->sik/dot_general | solution.py:43
  69.5 4.2 %multiply_convert_fusion = bf16[2,512,512]{2,1,0:T(8,128)(2,1)} fusion(bf16[2,512,512]{2,1,0:T(8,128)(2,1)} %convolution_convert_fusion.3, bf16[2,512,512]{2,1,0:T(8,128)(2,1)} %copy-done.5, f32[512,512]{1,0:T(8,128)S(1)} %copy-done.4), kind=kOutput, calls=%fused_computation.8 | convolution fusion | flops 1076887552 | bytes 4194304 | tf_op jit(solution)/shard_map/sij,sjk->sik/dot_general | solution.py:49
  73.7 2.3 %convolution_convert_fusion = bf16[2,512,512]{2,1,0:T(8,128)(2,1)S(1)} fusion(bf16[2,512,512]{2,1,0:T(8,128)(2,1)} %multiply_convert_fusion, bf16[2,512,512]{2,1,0:T(8,128)(2,1)} %copy-done.5, f32[512,512]{1,0:T(8,128)S(1)} %copy-done.4), kind=kOutput, calls=%fused_computation.11 | convolution fusion | flops 539492352 | bytes 4194304 | tf_op jit(solution)/shard_map/sij,sjk->sik/dot_general | solution.py:39
  76.0 1.0 copy-done.8
  77.0 2.5 %convolution_convert_fusion.4 = bf16[512,256]{1,0:T(8,128)(2,1)} fusion(bf16[2,512,512]{2,1,0:T(8,128)(2,1)} %copy-done.8, bf16[2,512,512]{2,1,0:T(8,128)(2,1)S(1)} %copy-done.1, s32[]{:T(128)S(6)} %select_n.116, bf16[1,512,512]{2,1,0:T(8,128)(2,1)S(1)} %slice.13, s32[]{:T(128)S(6)} %select_n.118), kind=kOutput, calls=%fused_computation.17 | convolution fusion | flops 268697600 | bytes 1572872 | tf_op jit(solution)/shard_map/dot_general | solution.py:90
  79.5 0.4 multiply_reduce_fusion.1
  79.9 16.6 %all-gather.5.cloned.1.call-done = bf16[512,1024]{1,0:T(8,128)(2,1)} async-done(((bf16[512,256]{1,0:T(8,128)(2,1)}), bf16[512,1024]{1,0:T(8,128)(2,1)}) %all-gather.5.cloned.1.call-update) | async-done | bytes 1048592 | tf_op jit(solution)/shard_map/all_gather | solution.py:93
  96.4 1.5 %multiply_reduce_fusion = f32[1024]{0:T(1024)S(1)} fusion(bf16[512,1024]{1,0:T(8,128)(2,1)} %all-gather.5.cloned.1.call-done), kind=kLoop, calls=%fused_computation.6 | loop fusion | flops 1571840 | bytes 1052672 | tf_op jit(solution)/shard_map/reduce_sum | solution.py:96
  97.9 1.8 %reshape.109 = bf16[512,2,512]{2,1,0:T(2,128)(2,1)S(1)} reshape(bf16[512,1024]{1,0:T(8,128)(2,1)} %all-gather.5.cloned.1.call-done) | data formatting | bytes 2097152 | tf_op jit(solution)/shard_map/reshape | solution.py:94
  99.8 0.2 constant_dynamic-slice_fusion
  100.0 0.1 reduce_sum.38
  100.1 0.1 multiply_convert_fusion.3
  100.2 0.7 copy.33
  101.0 5.5 %all-to-all-start.1 = ((bf16[8,64,2,128]{3,1,2,0:T(8,128)(2,1)}), bf16[8,64,2,128]{3,1,2,0:T(8,128)(2,1)S(1)}, u32[]{:S(2)}, u32[]{:S(2)}) async-start(bf16[8,64,2,128]{3,1,2,0:T(8,128)(2,1)} %copy.33), calls=%async_computation.1 | async-start | bytes 524288 | tf_op jit(solution)/shard_map/all_to_all | solution.py:101
  106.5 0.1 copy.34
  106.6 0.1 reshape.111
  106.6 0.6 scatter_custom_fusion
  107.3 1.0 copy.35
  108.3 7.5 %all-to-all-done.1 = bf16[8,64,2,128]{3,1,2,0:T(8,128)(2,1)S(1)} async-done(((bf16[8,64,2,128]{3,1,2,0:T(8,128)(2,1)}), bf16[8,64,2,128]{3,1,2,0:T(8,128)(2,1)S(1)}, u32[]{:S(2)}, u32[]{:S(2)}) %all-to-all-start.1) | async-done | bytes 262176 | tf_op jit(solution)/shard_map/all_to_all | solution.py:101
  115.8 1.3 %gather_fusion.1 = bf16[16,64,128]{2,1,0:T(8,128)(2,1)} fusion(bf16[8,64,2,128]{3,1,2,0:T(8,128)(2,1)S(1)} %all-to-all-done.1, s32[16]{0:T(128)S(1)} %fusion.19), kind=kCustom, calls=%fused_computation.1 | custom fusion | bytes 524416 | tf_op jit(solution)/shard_map/gather | solution.py:110
  (45 shorter events, 0.5 us)
Async XLA Ops:
  7.2 1.8 %copy-start = (bf16[16,64,128]{2,1,0:T(8,128)(2,1)S(1)}, bf16[16,64,128]{2,1,0:T(8,128)(2,1)}, u32[]{:S(2)}) copy-start(bf16[16,64,128]{2,1,0:T(8,128)(2,1)} %param.4) | copy-start | bytes 786436
  7.2 36.8 %all-gather.3.cloned.1.call-start = ((), (), s32[]{:S(2)}) async-start(), calls=%async_computation.2 | async-start | bytes 1310720 | tf_op jit(solution)/shard_map/all_gather | solution.py:73
  9.8 8.9 %collective-permute-start = (bf16[2,1,64,128]{3,2,1,0:T(8,128)(2,1)S(1)}, bf16[2,1,64,128]{3,2,1,0:T(8,128)(2,1)S(1)}, u32[]{:S(2)}, u32[]{:S(2)}) collective-permute-start(bf16[2,1,64,128]{3,2,1,0:T(8,128)(2,1)S(1)} %get-tuple-element.22), channel_id=1, source_target_pairs={{0,4},{4,0},{8,12},{12,8},{16,20},{20,16},{24,28},{28,24},{1,5},{5... | collective-permute-start | bytes 98312 | tf_op jit(solution)/shard_map/ppermute | solution.py:22
  12.8 9.5 %collective-permute-start.1 = (bf16[2,1,64,128]{3,2,1,0:T(8,128)(2,1)S(1)}, bf16[2,1,64,128]{3,2,1,0:T(8,128)(2,1)S(1)}, u32[]{:S(2)}, u32[]{:S(2)}) collective-permute-start(bf16[2,1,64,128]{3,2,1,0:T(8,128)(2,1)S(1)} %get-tuple-element.21), channel_id=1, source_target_pairs={{0,8},{4,12},{8,0},{12,4},{16,24},{20,28},{24,16},{28,20},{1,9},{5... | collective-permute-start | bytes 98312 | tf_op jit(solution)/shard_map/ppermute | solution.py:22
  14.4 8.0 %collective-permute-start.2 = (bf16[2,1,64,128]{3,2,1,0:T(8,128)(2,1)S(1)}, bf16[2,1,64,128]{3,2,1,0:T(8,128)(2,1)S(1)}, u32[]{:S(2)}, u32[]{:S(2)}) collective-permute-start(bf16[2,1,64,128]{3,2,1,0:T(8,128)(2,1)S(1)} %get-tuple-element.20), channel_id=1, source_target_pairs={{0,12},{4,8},{8,4},{12,0},{16,28},{20,24},{24,20},{28,16},{1,13},{... | collective-permute-start | bytes 98312 | tf_op jit(solution)/shard_map/ppermute | solution.py:22
  14.4 8.0 %collective-permute-start.3 = (bf16[2,1,64,128]{3,2,1,0:T(8,128)(2,1)S(1)}, bf16[2,1,64,128]{3,2,1,0:T(8,128)(2,1)S(1)}, u32[]{:S(2)}, u32[]{:S(2)}) collective-permute-start(bf16[2,1,64,128]{3,2,1,0:T(8,128)(2,1)S(1)} %get-tuple-element.19), channel_id=1, source_target_pairs={{0,16},{4,20},{8,24},{12,28},{16,0},{20,4},{24,8},{28,12},{1,17},{... | collective-permute-start | bytes 98312 | tf_op jit(solution)/shard_map/ppermute | solution.py:22
  17.4 5.8 %collective-permute-start.4 = (bf16[2,1,64,128]{3,2,1,0:T(8,128)(2,1)S(1)}, bf16[2,1,64,128]{3,2,1,0:T(8,128)(2,1)S(1)}, u32[]{:S(2)}, u32[]{:S(2)}) collective-permute-start(bf16[2,1,64,128]{3,2,1,0:T(8,128)(2,1)S(1)} %get-tuple-element.18), channel_id=1, source_target_pairs={{0,20},{4,16},{8,28},{12,24},{16,4},{20,0},{24,12},{28,8},{1,21},{... | collective-permute-start | bytes 98312 | tf_op jit(solution)/shard_map/ppermute | solution.py:22
  18.7 5.8 %collective-permute-start.5 = (bf16[2,1,64,128]{3,2,1,0:T(8,128)(2,1)S(1)}, bf16[2,1,64,128]{3,2,1,0:T(8,128)(2,1)S(1)}, u32[]{:S(2)}, u32[]{:S(2)}) collective-permute-start(bf16[2,1,64,128]{3,2,1,0:T(8,128)(2,1)S(1)} %get-tuple-element.17), channel_id=1, source_target_pairs={{0,24},{4,28},{8,16},{12,20},{16,8},{20,12},{24,0},{28,4},{1,25},{... | collective-permute-start | bytes 98312 | tf_op jit(solution)/shard_map/ppermute | solution.py:22
  22.3 6.7 %collective-permute-start.6 = (bf16[2,1,64,128]{3,2,1,0:T(8,128)(2,1)S(1)}, bf16[2,1,64,128]{3,2,1,0:T(8,128)(2,1)S(1)}, u32[]{:S(2)}, u32[]{:S(2)}) collective-permute-start(bf16[2,1,64,128]{3,2,1,0:T(8,128)(2,1)S(1)} %get-tuple-element.16), channel_id=1, source_target_pairs={{0,28},{4,24},{8,20},{12,16},{16,12},{20,8},{24,4},{28,0},{1,29},{... | collective-permute-start | bytes 98312 | tf_op jit(solution)/shard_map/ppermute | solution.py:22
  22.4 23.8 %copy-start.6 = (f32[2,2,128,512]{3,2,1,0:T(8,128)S(1)}, f32[2,2,128,512]{3,2,1,0:T(8,128)}, u32[]{:S(2)}) copy-start(f32[2,2,128,512]{3,2,1,0:T(8,128)} %param.5) | copy-start | bytes 3145732
  29.0 0.7 copy-start.2
  44.0 1.8 %copy-start.1 = (bf16[2,512,512]{2,1,0:T(8,128)(2,1)S(1)}, bf16[2,512,512]{2,1,0:T(8,128)(2,1)}, u32[]{:S(2)}) copy-start(bf16[2,512,512]{2,1,0:T(8,128)(2,1)} %all-gather.3.cloned.1.call-done) | copy-start | bytes 3145732
  44.0 2.3 %copy-start.7 = (f32[128,512]{1,0:T(8,128)S(1)}, f32[128,512]{1,0:T(8,128)}, u32[]{:S(2)}) copy-start(f32[128,512]{1,0:T(8,128)} %fusion.12) | copy-start | bytes 786436
  47.7 17.9 %all-to-all-start = ((bf16[4,2,128,512]{3,2,1,0:T(8,128)(2,1)}), bf16[4,2,128,512]{3,2,1,0:T(8,128)(2,1)S(1)}, u32[]{:S(2)}, u32[]{:S(2)}) async-start(bf16[4,2,128,512]{3,2,1,0:T(8,128)(2,1)} %bitcast.6), calls=%async_computation | async-start | bytes 2097152 | tf_op jit(solution)/shard_map/all_to_all | solution.py:83
  51.2 45.2 %all-gather.5.cloned.1.call-start = ((), (), s32[]{:S(2)}) async-start(), calls=%async_computation.3 | async-start | bytes 1310720 | tf_op jit(solution)/shard_map/all_gather | solution.py:93
  66.1 1.7 %copy-start.3 = (f32[512,512]{1,0:T(8,128)S(1)}, f32[512,512]{1,0:T(8,128)}, u32[]{:S(2)}) copy-start(f32[512,512]{1,0:T(8,128)} %fusion.2) | copy-start | bytes 3145732
  66.8 1.0 copy-start.5
  67.8 1.7 %copy-start.4 = (f32[512,512]{1,0:T(8,128)S(1)}, f32[512,512]{1,0:T(8,128)}, u32[]{:S(2)}) copy-start(f32[512,512]{1,0:T(8,128)} %fusion.2) | copy-start | bytes 3145732
  75.9 1.0 copy-start.8
  101.0 14.8 %all-to-all-start.1 = ((bf16[8,64,2,128]{3,1,2,0:T(8,128)(2,1)}), bf16[8,64,2,128]{3,1,2,0:T(8,128)(2,1)S(1)}, u32[]{:S(2)}, u32[]{:S(2)}) async-start(bf16[8,64,2,128]{3,1,2,0:T(8,128)(2,1)} %copy.33), calls=%async_computation.1 | async-start | bytes 524288 | tf_op jit(solution)/shard_map/all_to_all | solution.py:101
Sparse Core Ops, SparseCore 0:
  29.8 14.0 all-gather.2
  79.6 16.8 all-gather.4
